TPU v7x, 32 devices: a whole 2x2x4 slice. The times are simulated.
32 devices in a mesh: dp: 8 (over y, x, core), mp: 4 (over z).
Axes of the slice: x: 2, y: 2, z: 4, core: 2. Of those that a mesh axis runs over, the one named last changes fastest.
Arguments:
- attn_out: bfloat16 [8192, 8192], P('dp', 'mp'), may hold values from -6 to 6
- out_weight: bfloat16 [8192, 8192], P('dp'), may hold values from -0.09375 to 0.09375
- residual: bfloat16 [8, 1024, 8192], P(None, 'mp', 'dp'), may hold values from -6 to 6
Outputs:
- layer_out: bfloat16 [8, 1024, 8192], P(None, 'mp', 'dp')
All inputs are finite; a program needn't handle non-finite values.
Results may differ from a plain program's by a relative error of at most 0.001.
Values may be sent and summed in bfloat16 or wider, within the bound.
A program may use at most 192 MiB of HBM per device.

v0:
```python
import jax
import jax.numpy as jnp
from jax import lax
from jax.sharding import PartitionSpec as P


def shards(attn_out, out_weight, residual):
    by_rows = lax.all_to_all(attn_out, "mp", split_axis=0, concat_axis=1, tiled=True)
    columns = lax.all_to_all(out_weight, "dp", split_axis=1, concat_axis=0, tiled=True)
    projected = jnp.dot(
        lax.all_gather(by_rows, "dp", axis=0, tiled=True),
        columns,
        preferred_element_type=jnp.float32,
    )
    layer_out = residual.astype(jnp.float32) + projected.reshape(residual.shape)
    return layer_out.astype(jnp.bfloat16)


def solution(mesh):
    return jax.shard_map(
        shards,
        mesh=mesh,
        in_specs=(P("dp", "mp"), P("dp", None), P(None, "mp", "dp")),
        out_specs=P(None, "mp", "dp"),
        check_vma=False,
    )
```

profile of v0, /device:TPU:0, one launch (start us, length us, event | category | flops | bytes accessed | tf_op | source)
XLA Modules:
  0.0 492.3 jit_solution(1192712560543331920)
XLA Ops:
  6.5 0.0 all-gather.2.cloned.1.call-start
  6.5 99.5 %all_to_all.38 = bf16[4,256,2048]{2,1,0:T(8,128)(2,1)S(1)} all-to-all(bf16[4,256,2048]{2,1,0:T(8,128)(2,1)} %bitcast.21), channel_id=1, replica_groups=mesh['dp'=8,'mp'=4] {'mp'}, dimensions={0} | all-to-all | bytes 8388608 | tf_op jit(solution)/shard_map/all_to_all | solution.py:8
  106.0 2.3 copy.7
  108.3 0.0 all-gather.2.cloned.1.call-update
  108.4 9.0 %copy.9 = bf16[128,8,8,1024]{3,2,0,1:T(8,128)(2,1)S(1)} copy(bf16[128,8,8,1024]{3,2,1,0:T(8,128)(2,1)} %bitcast.17) | data formatting | bytes 33554432 | tf_op jit(solution)/shard_map/all_to_all | solution.py:9
  117.4 312.1 %all_to_all.39 = bf16[1024,8,1024]{2,0,1:T(8,128)(2,1)} all-to-all(bf16[1024,8,1024]{2,0,1:T(8,128)(2,1)S(1)} %bitcast.16), channel_id=1, replica_groups=mesh['dp'=8,'mp'=4] {'dp'}, dimensions={1} | all-to-all | bytes 33554432 | tf_op jit(solution)/shard_map/all_to_all | solution.py:9
  429.5 11.2 %all-gather.2.cloned.1.call-done = bf16[2048,8192]{1,0:T(8,128)(2,1)} async-done(((bf16[256,8192]{1,0:T(8,128)(2,1)}), bf16[2048,8192]{1,0:T(8,128)(2,1)}) %all-gather.2.cloned.1.call-update) | async-done | bytes 33554448 | tf_op jit(solution)/shard_map/all_gather | solution.py:11
  440.7 44.7 %add_convert_fusion = bf16[8,256,1024]{2,1,0:T(8,128)(2,1)} fusion(bf16[8,256,1024]{2,1,0:T(8,128)(2,1)} %param.5, bf16[8,256,8192]{2,1,0:T(8,128)(2,1)} %bitcast.22, bf16[8192,1024,1]{1,0,2:T(8,128)(2,1)} %bitcast.18), kind=kOutput, calls=%fused_computation.1 | convolution fusion | flops 34366029824 | bytes 58720256 | tf_op jit(solution)/shard_map/dot_general | solution.py:10
Async XLA Ops:
  6.5 434.2 %all-gather.2.cloned.1.call-start = ((), (), s32[]{:S(2)}) async-start(), calls=%async_computation.2 | async-start | bytes 37748736 | tf_op jit(solution)/shard_map/all_gather | solution.py:11
Sparse Core Ops, SparseCore 0:
  108.5 332.2 all-gather.1
where the time goes:
time: 493 us; the launch traced here: 492 us
  blocking collectives  412 us (84%)
  matrix products  44.7 us (9%)
  between operations  13.4 us (3%)
  local copies, waits for them, and re-layouts  11.3 us (2%)
  waiting for transfers between devices  11.2 us (2%)
    all_to_all x1, blocking collectives, shards(): lax.all_to_all(out_weight, 'dp', split_axis=1, concat_axis=0, tiled=True)  312 us
    all_to_all x1, blocking collectives, shards(): lax.all_to_all(attn_out, 'mp', split_axis=0, concat_axis=1, tiled=True)  99.5 us
    dot_general x1, matrix products, shards(): jnp.dot(lax.all_gather(by_rows, 'dp', axis=0, tiled=True), columns, prefe...  44.7 us
    all_gather x1, waiting for transfers between devices, shards(): lax.all_gather(by_rows, 'dp', axis=0, tiled=True)  11.2 us
  transfers between devices with their start and end apart: 1, of which 1 were waited for; matrix products, arithmetic and copies ran while one was open for 2% of the time, Pallas kernels for 0%

commit v1 on v0

--- a/solution.py
+++ b/solution.py
@@ -5,7 +5,10 @@
 
 
 def shards(attn_out, out_weight, residual):
-    by_rows = lax.all_to_all(attn_out, "mp", split_axis=0, concat_axis=1, tiled=True)
+    by_rows = jnp.concatenate(
+        lax.all_to_all(jnp.stack(jnp.split(attn_out, lax.axis_size("mp"), axis=0)), "mp", 0, 0),
+        axis=1,
+    )
     columns = lax.all_to_all(out_weight, "dp", split_axis=1, concat_axis=0, tiled=True)
     projected = jnp.dot(
         lax.all_gather(by_rows, "dp", axis=0, tiled=True),

time: 493 us -> 550 us (1.12)
  blocking collectives: 412 us -> 99.4 us
  waiting for transfers between devices: 11.2 us -> 319 us
  local copies, waits for them, and re-layouts: 11.3 us -> 64.5 us
  starting transfers between devices: 0.01 us -> 5.82 us
    all_to_all x2 -> x1, blocking collectives: 412 us -> 99.4 us  [shards(): lax.all_to_all(jnp.stack(jnp.split(attn_out, lax.axis_size('mp'), axis=0)...]
    all_gather x1, waiting for transfers between devices: 11.2 us -> 319 us  [shards(): lax.all_gather(by_rows, 'dp', axis=0, tiled=True)]
    all_gather x0 -> x1, local copies, waits for them, and re-layouts: none -> 40.5 us  [shards(): lax.all_gather(by_rows, 'dp', axis=0, tiled=True)]
    all_to_all x0 -> x1, starting transfers between devices: none -> 5.81 us  [shards(): lax.all_to_all(out_weight, 'dp', split_axis=1, concat_axis=0, tiled=True)]
    unnamed x0 -> x4, local copies, waits for them, and re-layouts: none -> 5.57 us
    all_to_all x1, local copies, waits for them, and re-layouts: 9.01 us -> 14.5 us  [shards(): lax.all_to_all(out_weight, 'dp', split_axis=1, concat_axis=0, tiled=True)]
  transfers between devices with their start and end apart: 1 -> 2, of which waited for: 1 -> 1; matrix products, arithmetic and copies ran while one was open for 2% -> 10% of each run, Pallas kernels for 0% -> 0%
where the time goes in v1:
time: 550 us; the launch traced here: 548 us
  waiting for transfers between devices  319 us (58%)
  blocking collectives  99.4 us (18%)
  local copies, waits for them, and re-layouts  64.5 us (12%)
  matrix products  44.7 us (8%)
  between operations  13.4 us (2%)
  starting transfers between devices  5.82 us (1%)
    all_gather x1, waiting for transfers between devices, shards(): lax.all_gather(by_rows, 'dp', axis=0, tiled=True)  319 us
    all_to_all x1, blocking collectives, shards(): lax.all_to_all(jnp.stack(jnp.split(attn_out, lax.axis_size('mp'), axis=0)...  99.4 us
    dot_general x1, matrix products, shards(): jnp.dot(lax.all_gather(by_rows, 'dp', axis=0, tiled=True), columns, prefe...  44.7 us
    all_gather x1, local copies, waits for them, and re-layouts, shards(): lax.all_gather(by_rows, 'dp', axis=0, tiled=True)  40.5 us
    all_to_all x1, local copies, waits for them, and re-layouts, shards(): lax.all_to_all(out_weight, 'dp', split_axis=1, concat_axis=0, tiled=True)  14.5 us
  transfers between devices with their start and end apart: 2, of which 1 were waited for; matrix products, arithmetic and copies ran while one was open for 10% of the time, Pallas kernels for 0%

profile of v1, /device:TPU:0, one launch (start us, length us, event | category | flops | bytes accessed | tf_op | source)
XLA Modules:
  0.0 548.2 jit_solution(10985900626313082089)
XLA Ops:
  6.5 0.0 all-gather.2.cloned.1.call-start
  6.5 3.9 fusion
  10.5 0.5 copy.11
  11.0 1.5 copy.13
  12.5 2.3 copy.12
  14.8 1.3 copy.14
  16.1 1.8 pad_maximum_fusion
  17.9 99.4 %all_to_all.24 = bf16[4,256,2048]{1,2,0:T(8,128)(2,1)} all-to-all(bf16[4,256,2048]{1,2,0:T(8,128)(2,1)S(1)} %pad_maximum_fusion), channel_id=1, replica_groups=mesh['dp'=8,'mp'=4] {'mp'}, dimensions={0} | all-to-all | bytes 8388608 | tf_op jit(solution)/shard_map/all_to_all | solution.py:9
  117.3 0.0 all-gather.2.cloned.1.call-update
  117.3 14.5 %copy.17 = bf16[128,8,8,1024]{3,2,0,1:T(8,128)(2,1)} copy(bf16[128,8,8,1024]{3,2,1,0:T(8,128)(2,1)} %bitcast.21) | data formatting | bytes 33554432 | tf_op jit(solution)/shard_map/all_to_all | solution.py:12
  131.8 5.8 %all-to-all-start.1 = ((bf16[1024,8,1024]{2,0,1:T(8,128)(2,1)}), bf16[1024,8,1024]{2,0,1:T(8,128)(2,1)}, u32[]{:S(2)}, u32[]{:S(2)}) async-start(bf16[1024,8,1024]{2,0,1:T(8,128)(2,1)} %bitcast.19), calls=%async_computation.1 | async-start | bytes 33554432 | tf_op jit(solution)/shard_map/all_to_all | solution.py:12
  137.6 318.6 %all-gather.2.cloned.1.call-done = bf16[2048,8192]{0,1:T(8,128)(2,1)} async-done(((bf16[256,8192]{0,1:T(8,128)(2,1)}), bf16[2048,8192]{0,1:T(8,128)(2,1)}) %all-gather.2.cloned.1.call-update) | async-done | bytes 33554448 | tf_op jit(solution)/shard_map/all_gather | solution.py:14
  456.2 40.5 %copy.9 = bf16[2048,8192]{1,0:T(8,128)(2,1)} copy(bf16[2048,8192]{0,1:T(8,128)(2,1)} %all-gather.2.cloned.1.call-done) | data formatting | bytes 67108864 | tf_op jit(solution)/shard_map/all_gather | solution.py:14
  496.7 0.0 all-to-all-done.1
  496.7 44.7 %add_convert_fusion = bf16[8,256,1024]{2,1,0:T(8,128)(2,1)} fusion(bf16[8,256,1024]{2,1,0:T(8,128)(2,1)} %param.5, bf16[8,256,8192]{2,1,0:T(8,128)(2,1)} %bitcast.20, bf16[8192,1024,1]{1,0,2:T(8,128)(2,1)} %bitcast.9), kind=kOutput, calls=%fused_computation.1 | convolution fusion | flops 34366029824 | bytes 58720256 | tf_op jit(solution)/shard_map/dot_general | solution.py:13
Async XLA Ops:
  6.5 449.7 %all-gather.2.cloned.1.call-start = ((), (), s32[]{:S(2)}) async-start(), calls=%async_computation.2 | async-start | bytes 37748736 | tf_op jit(solution)/shard_map/all_gather | solution.py:14
  131.8 364.9 %all-to-all-start.1 = ((bf16[1024,8,1024]{2,0,1:T(8,128)(2,1)}), bf16[1024,8,1024]{2,0,1:T(8,128)(2,1)}, u32[]{:S(2)}, u32[]{:S(2)}) async-start(bf16[1024,8,1024]{2,0,1:T(8,128)(2,1)} %bitcast.19), calls=%async_computation.1 | async-start | bytes 33554432 | tf_op jit(solution)/shard_map/all_to_all | solution.py:12
Sparse Core Ops, SparseCore 0:
  117.4 338.7 all-gather.1
